TPU v7x, 16 devices: a whole 2x2x2 slice. The times are simulated.
16 devices in a mesh: tp: 4 (over z, y), dp: 4 (over x, core).
Axes of the slice: x: 2, y: 2, z: 2, core: 2. Of those that a mesh axis runs over, the one named last changes fastest.
Arguments:
- tokens: int32 [16, 1024], P('dp')
- labels: int32 [16, 1024], P('dp')
- embedding: float32 [50304, 512], P('tp')
- vec_params: float32 [16, 512], replicated
- w_qkv: float32 [2, 512, 1536], P(None, None, 'tp')
- b_qkv: float32 [2, 8, 192], P(None, 'tp')
- w_out: float32 [2, 512, 512], P(None, 'tp')
- w_up: float32 [2, 512, 2048], P(None, None, 'tp')
- b_up: float32 [2, 2048], P(None, 'tp')
- w_down: float32 [2, 2048, 512], P(None, 'tp')
- mom_embedding: float32 [50304, 512], P('tp')
- mom_vec_params: float32 [16, 512], replicated
- mom_w_qkv: float32 [2, 512, 1536], P(None, None, 'tp')
- mom_b_qkv: float32 [2, 8, 192], P(None, 'tp')
- mom_w_out: float32 [2, 512, 512], P(None, 'tp')
- mom_w_up: float32 [2, 512, 2048], P(None, None, 'tp')
- mom_b_up: float32 [2, 2048], P(None, 'tp')
- mom_w_down: float32 [2, 2048, 512], P(None, 'tp')
- vel_embedding: float32 [50304, 512], P('tp')
- vel_vec_params: float32 [16, 512], replicated
- vel_w_qkv: float32 [2, 512, 1536], P(None, None, 'tp')
- vel_b_qkv: float32 [2, 8, 192], P(None, 'tp')
- vel_w_out: float32 [2, 512, 512], P(None, 'tp')
- vel_w_up: float32 [2, 512, 2048], P(None, None, 'tp')
- vel_b_up: float32 [2, 2048], P(None, 'tp')
- vel_w_down: float32 [2, 2048, 512], P(None, 'tp')
Outputs:
- output 1: float32 [], replicated
- output 2: float32 [50304, 512], P('tp')
- output 3: float32 [16, 512], replicated
- output 4: float32 [2, 512, 1536], P(None, None, 'tp')
- output 5: float32 [2, 8, 192], P(None, 'tp')
- output 6: float32 [2, 512, 512], P(None, 'tp')
- output 7: float32 [2, 512, 2048], P(None, None, 'tp')
- output 8: float32 [2, 2048], P(None, 'tp')
- output 9: float32 [2, 2048, 512], P(None, 'tp')
- output 10: float32 [50304, 512], P('tp')
- output 11: float32 [16, 512], replicated
- output 12: float32 [2, 512, 1536], P(None, None, 'tp')
- output 13: float32 [2, 8, 192], P(None, 'tp')
- output 14: float32 [2, 512, 512], P(None, 'tp')
- output 15: float32 [2, 512, 2048], P(None, None, 'tp')
- output 16: float32 [2, 2048], P(None, 'tp')
- output 17: float32 [2, 2048, 512], P(None, 'tp')
- output 18: float32 [50304, 512], P('tp')
- output 19: float32 [16, 512], replicated
- output 20: float32 [2, 512, 1536], P(None, None, 'tp')
- output 21: float32 [2, 8, 192], P(None, 'tp')
- output 22: float32 [2, 512, 512], P(None, 'tp')
- output 23: float32 [2, 512, 2048], P(None, None, 'tp')
- output 24: float32 [2, 2048], P(None, 'tp')
- output 25: float32 [2, 2048, 512], P(None, 'tp')
- output 26: bfloat16 [50304, 512], P('tp')
- output 27: bfloat16 [16, 512], replicated
- output 28: bfloat16 [2, 512, 1536], P(None, None, 'tp')
- output 29: bfloat16 [2, 8, 192], P(None, 'tp')
- output 30: bfloat16 [2, 512, 512], P(None, 'tp')
- output 31: bfloat16 [2, 512, 2048], P(None, None, 'tp')
- output 32: bfloat16 [2, 2048], P(None, 'tp')
- output 33: bfloat16 [2, 2048, 512], P(None, 'tp')
All inputs are finite; a program needn't handle non-finite values.
Results may differ from a plain program's by a relative error of at most 0.001.
Values sent between devices are 32-bit elements.
A program may use at most 1 GiB of HBM per device.

v0:
```python
import math
import jax
import jax.numpy as jnp
from jax import lax
from jax.sharding import PartitionSpec as P

LN_EPS = 1e-5
CLIP_NORM = 1.0
BETA_ONE = 0.9
BETA_TWO = 0.95
ADAM_EPS = 1e-8
WEIGHT_DECAY = 0.1
LEARN_RATE = 1e-3
STEP_COUNT = 10
DECAYED = (True, False, True, False, True, True, False, True)
PARAM_SPECS = (P('tp', None), P(None, None), P(None, None, 'tp'), P(None, 'tp', None), P(None, 'tp', None), P(None, None, 'tp'), P(None, 'tp'), P(None, 'tp', None))
CONTRACT_ROWS = (((0,), (0,)), ((), ()))
CONTRACT_COLS = (((1,), (1,)), ((), ()))


def alibi_slopes(heads):
    closest = 2 ** int(math.floor(math.log2(heads)))
    first_base = 2.0 ** (-8.0 / closest)
    slopes = [first_base ** (head_idx + 1) for head_idx in range(closest)]
    extra_base = 2.0 ** (-4.0 / closest)
    extra_count = min(closest, heads - closest)
    return slopes + [extra_base ** (2 * head_idx + 1) for head_idx in range(extra_count)]


def layer_norm(values, gain, bias):
    centred = values - jnp.mean(values, axis=-1, keepdims=True)
    variance = jnp.mean(centred * centred, axis=-1, keepdims=True)
    return centred * lax.rsqrt(variance + LN_EPS) * gain + bias


def gelu_tanh(values):
    return jax.nn.gelu(values, approximate=True)


def attn_probs(query, key_blk, slopes, scale):
    seq_len = query.shape[1]
    positions = jnp.arange(seq_len)
    rel_pos = (positions[None, :] - positions[:, None]).astype(jnp.float32)
    causal = positions[None, :] <= positions[:, None]
    scores = jnp.einsum('bqhd,bkhd->bhqk', query, key_blk, preferred_element_type=jnp.float32) * scale
    scores = scores + slopes[None, :, None, None] * rel_pos[None, None]
    scores = jnp.where(causal[None, None], scores, -jnp.inf)
    return jax.nn.softmax(scores, axis=-1)


def adam_update(master, grad_arr, moment, velocity, decayed):
    mom_new = BETA_ONE * moment + (1.0 - BETA_ONE) * grad_arr
    vel_new = BETA_TWO * velocity + (1.0 - BETA_TWO) * grad_arr * grad_arr
    mom_hat = mom_new / (1.0 - BETA_ONE ** STEP_COUNT)
    vel_hat = vel_new / (1.0 - BETA_TWO ** STEP_COUNT)
    direction = mom_hat / (jnp.sqrt(vel_hat) + ADAM_EPS)
    if decayed:
        direction = direction + WEIGHT_DECAY * master
    return master - LEARN_RATE * direction, mom_new, vel_new


def local_grads(tokens, labels, masters, tp_size, dp_size):
    embedding, vec_params, w_qkv, b_qkv, w_out, w_up, b_up, w_down = masters
    tp_rank = lax.axis_index('tp')
    vocab_loc = embedding.shape[0]
    batch_loc, seq_len = tokens.shape
    n_tok = batch_loc * seq_len
    n_total = n_tok * dp_size
    layers = w_qkv.shape[0]
    heads_loc = b_qkv.shape[1]
    head_dim = b_qkv.shape[2] // 3
    scale = head_dim ** -0.5
    slope_all = jnp.array(alibi_slopes(heads_loc * tp_size), dtype=jnp.float32)
    slope_loc = lax.dynamic_slice_in_dim(slope_all, tp_rank * heads_loc, heads_loc)
    emb_b = embedding.astype(jnp.bfloat16)
    wqkv_b = w_qkv.astype(jnp.bfloat16)
    wout_b = w_out.astype(jnp.bfloat16)
    wup_b = w_up.astype(jnp.bfloat16)
    wdown_b = w_down.astype(jnp.bfloat16)

    id_local = tokens.reshape(-1) - tp_rank * vocab_loc
    in_shard = (id_local >= 0) & (id_local < vocab_loc)
    safe_ids = jnp.clip(id_local, 0, vocab_loc - 1)
    picked = jnp.take(emb_b, safe_ids, axis=0)
    x_embed = lax.psum(jnp.where(in_shard[:, None], picked.astype(jnp.float32), 0.0), 'tp')
    resid, ln_zero_vjp = jax.vjp(layer_norm, x_embed, vec_params[0], vec_params[1])

    saved = []
    for layer in range(layers):
        row_base = 2 + 6 * layer
        normed_one, ln_one_vjp = jax.vjp(layer_norm, resid, vec_params[row_base], vec_params[row_base + 1])
        act_in = normed_one.astype(jnp.bfloat16)
        qkv = (jnp.dot(act_in, wqkv_b[layer], preferred_element_type=jnp.float32) + b_qkv[layer].reshape(-1)).astype(jnp.bfloat16)
        qkv = qkv.reshape(batch_loc, seq_len, heads_loc, 3, head_dim)
        query = qkv[:, :, :, 0]
        key_blk = qkv[:, :, :, 1]
        value_blk = qkv[:, :, :, 2]
        probs = attn_probs(query, key_blk, slope_loc, scale)
        context = jnp.einsum('bhqk,bkhd->bqhd', probs.astype(jnp.bfloat16), value_blk, preferred_element_type=jnp.float32).astype(jnp.bfloat16).reshape(n_tok, heads_loc * head_dim)
        attn_out = lax.psum(jnp.dot(context, wout_b[layer], preferred_element_type=jnp.float32), 'tp') + vec_params[row_base + 2]
        mid = resid + attn_out
        normed_two, ln_two_vjp = jax.vjp(layer_norm, mid, vec_params[row_base + 3], vec_params[row_base + 4])
        mlp_in = normed_two.astype(jnp.bfloat16)
        pre_act = jnp.dot(mlp_in, wup_b[layer], preferred_element_type=jnp.float32) + b_up[layer]
        act_out, gelu_vjp = jax.vjp(gelu_tanh, pre_act)
        hidden = act_out.astype(jnp.bfloat16)
        resid = mid + lax.psum(jnp.dot(hidden, wdown_b[layer], preferred_element_type=jnp.float32), 'tp') + vec_params[row_base + 5]
        saved.append((ln_one_vjp, act_in, query, key_blk, value_blk, context, ln_two_vjp, mlp_in, gelu_vjp, hidden))

    final_row = 2 + 6 * layers
    normed_fin, ln_fin_vjp = jax.vjp(layer_norm, resid, vec_params[final_row], vec_params[final_row + 1])
    head_in = normed_fin.astype(jnp.bfloat16)
    logits = lax.dot_general(head_in, emb_b, CONTRACT_COLS, preferred_element_type=jnp.float32)
    glob_max = lax.pmax(jnp.max(logits, axis=1), 'tp')
    shifted = jnp.exp(logits - glob_max[:, None])
    sum_exp = lax.psum(jnp.sum(shifted, axis=1), 'tp')
    lab_local = labels.reshape(-1) - tp_rank * vocab_loc
    onehot = jnp.arange(vocab_loc)[None, :] == lab_local[:, None]
    target = lax.psum(jnp.sum(jnp.where(onehot, logits, 0.0), axis=1), 'tp')
    loss_sum = jnp.sum(glob_max + jnp.log(sum_exp) - target)

    d_logits = ((shifted / sum_exp[:, None] - onehot.astype(jnp.float32)) / n_total).astype(jnp.bfloat16)
    g_emb = lax.dot_general(d_logits, head_in, CONTRACT_ROWS, preferred_element_type=jnp.float32)
    d_head = lax.psum(jnp.dot(d_logits, emb_b, preferred_element_type=jnp.float32), 'tp')
    vec_grads = {}
    d_resid, vec_grads[final_row], vec_grads[final_row + 1] = ln_fin_vjp(d_head)
    g_qkv_all = {}
    g_bqkv_all = {}
    g_out_all = {}
    g_up_all = {}
    g_bup_all = {}
    g_down_all = {}
    for layer in reversed(range(layers)):
        ln_one_vjp, act_in, query, key_blk, value_blk, context, ln_two_vjp, mlp_in, gelu_vjp, hidden = saved[layer]
        row_base = 2 + 6 * layer
        vec_grads[row_base + 5] = jnp.sum(d_resid, axis=0)
        d_out = d_resid.astype(jnp.bfloat16)
        g_down_all[layer] = lax.dot_general(hidden, d_out, CONTRACT_ROWS, preferred_element_type=jnp.float32)
        d_hidden = lax.dot_general(d_out, wdown_b[layer], CONTRACT_COLS, preferred_element_type=jnp.float32)
        d_pre = gelu_vjp(d_hidden)[0]
        g_bup_all[layer] = jnp.sum(d_pre, axis=0)
        d_pre_b = d_pre.astype(jnp.bfloat16)
        g_up_all[layer] = lax.dot_general(mlp_in, d_pre_b, CONTRACT_ROWS, preferred_element_type=jnp.float32)
        d_norm_two = lax.psum(lax.dot_general(d_pre_b, wup_b[layer], CONTRACT_COLS, preferred_element_type=jnp.float32), 'tp')
        d_mid_ln, vec_grads[row_base + 3], vec_grads[row_base + 4] = ln_two_vjp(d_norm_two)
        d_mid = d_resid + d_mid_ln
        vec_grads[row_base + 2] = jnp.sum(d_mid, axis=0)
        d_attn = d_mid.astype(jnp.bfloat16)
        g_out_all[layer] = lax.dot_general(context, d_attn, CONTRACT_ROWS, preferred_element_type=jnp.float32)
        d_context = lax.dot_general(d_attn, wout_b[layer], CONTRACT_COLS, preferred_element_type=jnp.float32).astype(jnp.bfloat16).reshape(batch_loc, seq_len, heads_loc, head_dim)
        probs = attn_probs(query, key_blk, slope_loc, scale)
        d_probs = jnp.einsum('bqhd,bkhd->bhqk', d_context, value_blk, preferred_element_type=jnp.float32)
        d_value = jnp.einsum('bhqk,bqhd->bkhd', probs.astype(jnp.bfloat16), d_context, preferred_element_type=jnp.float32)
        d_scores = (probs * (d_probs - jnp.sum(probs * d_probs, axis=-1, keepdims=True)) * scale).astype(jnp.bfloat16)
        d_query = jnp.einsum('bhqk,bkhd->bqhd', d_scores, key_blk, preferred_element_type=jnp.float32)
        d_key = jnp.einsum('bhqk,bqhd->bkhd', d_scores, query, preferred_element_type=jnp.float32)
        d_qkv = jnp.stack([d_query, d_key, d_value], axis=3).reshape(n_tok, heads_loc * 3 * head_dim)
        g_bqkv_all[layer] = jnp.sum(d_qkv, axis=0).reshape(heads_loc, 3 * head_dim)
        d_qkv_b = d_qkv.astype(jnp.bfloat16)
        g_qkv_all[layer] = lax.dot_general(act_in, d_qkv_b, CONTRACT_ROWS, preferred_element_type=jnp.float32)
        d_norm_one = lax.psum(lax.dot_general(d_qkv_b, wqkv_b[layer], CONTRACT_COLS, preferred_element_type=jnp.float32), 'tp')
        d_res_ln, vec_grads[row_base], vec_grads[row_base + 1] = ln_one_vjp(d_norm_one)
        d_resid = d_mid + d_res_ln
    d_embed, vec_grads[0], vec_grads[1] = ln_zero_vjp(d_resid)
    d_rows = jnp.where(in_shard[:, None], d_embed, 0.0)
    g_emb = g_emb + jax.ops.segment_sum(d_rows, safe_ids, num_segments=vocab_loc)
    grads = [g_emb,
             jnp.stack([vec_grads[row] for row in range(final_row + 2)]),
             jnp.stack([g_qkv_all[layer] for layer in range(layers)]),
             jnp.stack([g_bqkv_all[layer] for layer in range(layers)]),
             jnp.stack([g_out_all[layer] for layer in range(layers)]),
             jnp.stack([g_up_all[layer] for layer in range(layers)]),
             jnp.stack([g_bup_all[layer] for layer in range(layers)]),
             jnp.stack([g_down_all[layer] for layer in range(layers)])]
    return loss_sum, grads


def solution(mesh):
    tp_size = mesh.shape['tp']
    dp_size = mesh.shape['dp']

    def device_step(tokens, labels, *state):
        masters = state[0:8]
        moms = state[8:16]
        vels = state[16:24]
        loss_sum, grads = local_grads(tokens, labels, masters, tp_size, dp_size)
        n_total = tokens.shape[0] * tokens.shape[1] * dp_size
        loss = lax.psum(loss_sum, 'dp') / n_total
        grads = [lax.psum(grad_arr, 'dp') for grad_arr in grads]
        sq_sharded = sum(jnp.sum(grads[slot] * grads[slot]) for slot in range(8) if slot != 1)
        sq_total = lax.psum(sq_sharded, 'tp') + jnp.sum(grads[1] * grads[1])
        clip_coef = jnp.minimum(1.0, CLIP_NORM / (jnp.sqrt(sq_total) + 1e-6))
        updated = [adam_update(masters[slot], grads[slot] * clip_coef, moms[slot], vels[slot], DECAYED[slot]) for slot in range(8)]
        new_masters = [entry[0] for entry in updated]
        new_moms = [entry[1] for entry in updated]
        new_vels = [entry[2] for entry in updated]
        new_bf16 = [entry.astype(jnp.bfloat16) for entry in new_masters]
        return (loss, *new_masters, *new_moms, *new_vels, *new_bf16)

    data_spec = P('dp', None)
    return jax.shard_map(device_step, mesh=mesh, in_specs=(data_spec, data_spec) + PARAM_SPECS * 3, out_specs=(P(),) + PARAM_SPECS * 4, check_vma=False)
```

profile of v0, /device:TPU:0, one launch (start us, length us, event | category | flops | bytes accessed | tf_op | source)
XLA Modules:
  0.0 3367.0 jit_solution(4141828035407128113)
XLA Ops:
  22.3 23.8 gather_fusion
  62.9 158.4 %all-reduce.15.cloned.1.call-done = f32[4096,512]{1,0:T(8,128)} async-done(((f32[4096,512]{1,0:T(8,128)}), f32[4096,512]{1,0:T(8,128)}) %all-reduce.15.cloned.1.call-update) | async-done | bytes 8388624 | tf_op jit(solution)/shard_map/psum | solution.py:85
  302.0 162.5 %all-reduce.17.cloned.1.call-done = f32[4096,512]{1,0:T(8,128)} async-done(((f32[4096,512]{1,0:T(8,128)}), f32[4096,512]{1,0:T(8,128)}) %all-reduce.17.cloned.1.call-update) | async-done | bytes 8388624 | tf_op jit(solution)/shard_map/psum | solution.py:100
  487.1 164.8 %all-reduce.19.cloned.1.call-done = f32[4096,512]{1,0:T(8,128)} async-done(((f32[4096,512]{1,0:T(8,128)}), f32[4096,512]{1,0:T(8,128)}) %all-reduce.19.cloned.1.call-update) | async-done | bytes 8388624 | tf_op jit(solution)/shard_map/psum | solution.py:107
  685.0 20.7 fusion.209
  725.2 164.8 %all-reduce.21.cloned.1.call-done = f32[4096,512]{1,0:T(8,128)} async-done(((f32[4096,512]{1,0:T(8,128)}), f32[4096,512]{1,0:T(8,128)}) %all-reduce.21.cloned.1.call-update) | async-done | bytes 8388624 | tf_op jit(solution)/shard_map/psum | solution.py:100
  922.0 164.2 %all-reduce.23.cloned.1.call-done = f32[4096,512]{1,0:T(8,128)} async-done(((f32[4096,512]{1,0:T(8,128)}), f32[4096,512]{1,0:T(8,128)}) %all-reduce.23.cloned.1.call-update) | async-done | bytes 8388624 | tf_op jit(solution)/shard_map/psum | solution.py:107
  1104.9 75.9 %fusion.210 = (f32[4096]{0:T(1024)S(1)}, f32[4096,12576]{0,1:T(8,128)}) fusion(bf16[12576,512]{1,0:T(8,128)(2,1)} %convert_element_type.161, bf16[4096,512]{1,0:T(8,128)(2,1)} %add_convert_fusion.11.clone.4), kind=kOutput, calls=%fused_computation.321 | convolution fusion | flops 52799074304 | bytes 223133696 | tf_op jit(solution)/shard_map/dot_general | solution.py:113
  1196.5 62.5 %fusion.4 = (f32[4096]{0:T(1024)S(1)}, f32[4096]{0:T(1024)S(1)}) fusion(f32[4096,12576]{0,1:T(8,128)} %get-tuple-element.157, f32[4096]{0:T(1024)S(1)} %pmax.7, s32[4096]{0:T(1024)S(1)} %bitcast.292), kind=kLoop, calls=%fused_computation.10 | loop fusion | flops 257548288 | bytes 206110720 | tf_op jit(solution)/shard_map/reduce_sum | solution.py:116
  1274.2 98.2 %multiply_convert_fusion = bf16[4096,12576]{0,1:T(8,128)(2,1)} fusion(f32[4096,12576]{0,1:T(8,128)} %get-tuple-element.157, f32[4096]{0:T(1024)S(1)} %get-tuple-element.63, s32[4096]{0:T(1024)S(1)} %bitcast.293, f32[4096]{0:T(1024)S(1)} %pmax.7), kind=kLoop, calls=%fused_computation.6 | loop fusion | flops 360579072 | bytes 309116928 | tf_op jit(solution)/shard_map/convert_element_type | solution.py:122
  1372.4 64.9 %fusion.213 = f32[4096,512]{1,0:T(8,128)} fusion(bf16[4096,12576]{0,1:T(8,128)(2,1)} %multiply_convert_fusion, bf16[12576,512]{1,0:T(8,128)(2,1)} %convert_element_type.161), kind=kOutput, calls=%fused_computation.324 | convolution fusion | flops 52747567104 | bytes 124289024 | tf_op jit(solution)/shard_map/dot_general | solution.py:124
  1437.4 164.5 %all-reduce.25.cloned.1.call-done = f32[4096,512]{1,0:T(8,128)} async-done(((f32[4096,512]{1,0:T(8,128)}), f32[4096,512]{1,0:T(8,128)}) %all-reduce.25.cloned.1.call-update) | async-done | bytes 8388624 | tf_op jit(solution)/shard_map/psum | solution.py:124
  1633.1 164.8 %all-reduce.27.cloned.1.call-done = f32[4096,512]{1,0:T(8,128)} async-done(((f32[4096,512]{1,0:T(8,128)}), f32[4096,512]{1,0:T(8,128)}) %all-reduce.27.cloned.1.call-update) | async-done | bytes 8388624 | tf_op jit(solution)/shard_map/psum | solution.py:144
  1850.1 43.7 %fusion.105 = f32[4,1024,2,1,64]{1,4,2,0,3:T(8,128)} fusion(f32[4,2,1024,1024]{2,3,1,0:T(8,128)} %fusion.137, bf16[4,1024,2,1,64]{1,0,4,3,2:T(4,128)(2,1)} %get-tuple-element.125, f32[4,2,1024,1024]{2,3,1,0:T(8,128)} %get-tuple-element.155, f32[4,2,1024]{2,1,0:T(2,128)S(1)} %copy-done.177), kind=kOutput, calls=%fused_computation.166 | convolution fusion | flops 1132471296 | bytes 70287360 | tf_op jit(solution)/shard_map/bhqk,bqhd->bkhd/dot_general | solution.py:156
  1893.8 43.5 %fusion.102 = f32[4,1024,2,1,64]{1,4,2,0,3:T(8,128)} fusion(f32[4,2,1024,1024]{2,3,1,0:T(8,128)} %fusion.137, bf16[4,1024,2,1,64]{1,0,4,3,2:T(4,128)(2,1)S(1)} %copy-done.74, f32[4,2,1024,1024]{2,3,1,0:T(8,128)} %get-tuple-element.155, f32[4,2,1024]{2,1,0:T(2,128)S(1)} %copy-done.177), kind=kOutput, calls=%fused_computation.165 | convolution fusion | flops 1132471296 | bytes 70287360 | tf_op jit(solution)/shard_map/bhqk,bkhd->bqhd/dot_general | solution.py:155
  1951.7 164.8 %all-reduce.29.cloned.1.call-done = f32[4096,512]{1,0:T(8,128)} async-done(((f32[4096,512]{1,0:T(8,128)}), f32[4096,512]{1,0:T(8,128)}) %all-reduce.29.cloned.1.call-update) | async-done | bytes 8388624 | tf_op jit(solution)/shard_map/psum | solution.py:161
  2153.7 164.2 %all-reduce.31.cloned.1.call-done = f32[4096,512]{1,0:T(8,128)} async-done(((f32[4096,512]{1,0:T(8,128)}), f32[4096,512]{1,0:T(8,128)}) %all-reduce.31.cloned.1.call-update) | async-done | bytes 8388624 | tf_op jit(solution)/shard_map/psum | solution.py:144
  2369.5 43.7 %fusion.99 = f32[4,1024,2,1,64]{1,4,2,0,3:T(8,128)} fusion(f32[4,2,1024,1024]{2,3,1,0:T(8,128)} %fusion.136, bf16[4,1024,2,1,64]{1,0,4,3,2:T(4,128)(2,1)} %get-tuple-element.128, f32[4,2,1024,1024]{2,3,1,0:T(8,128)} %get-tuple-element.153, f32[4,2,1024]{2,1,0:T(2,128)S(1)} %copy-done.175), kind=kOutput, calls=%fused_computation.164 | convolution fusion | flops 1132471296 | bytes 70287360 | tf_op jit(solution)/shard_map/bhqk,bqhd->bkhd/dot_general | solution.py:156
  2413.1 43.4 %fusion.96 = f32[4,1024,2,1,64]{1,4,2,0,3:T(8,128)} fusion(f32[4,2,1024,1024]{2,3,1,0:T(8,128)} %fusion.136, bf16[4,1024,2,1,64]{1,0,4,3,2:T(4,128)(2,1)S(1)} %copy-done.73, f32[4,2,1024,1024]{2,3,1,0:T(8,128)} %get-tuple-element.153, f32[4,2,1024]{2,1,0:T(2,128)S(1)} %copy-done.175), kind=kOutput, calls=%fused_computation.163 | convolution fusion | flops 1132471296 | bytes 70287360 | tf_op jit(solution)/shard_map/bhqk,bkhd->bqhd/dot_general | solution.py:155
  2470.7 66.0 %fusion.171 = f32[12576,512]{1,0:T(8,128)} fusion(bf16[4096,12576]{0,1:T(8,128)(2,1)} %multiply_convert_fusion, f32[4096,512]{1,0:T(8,128)} %get-tuple-element.116, f32[512]{0:T(512)S(1)} %bitcast.322, f32[512]{0:T(512)S(1)} %bitcast.307, f32[4096]{0:T(1024)S(1)} %copy-done.94, f32[4096]{0:T(1024)S(1)} %copy-done.81), kind=kOutput, calls=%fused_computation.290 | convolution fusion | flops 52758052864 | bytes 137203712 | tf_op jit(solution)/shard_map/dot_general | solution.py:123
  2573.7 61.8 %all-reduce.33.cloned.1.call-done = f32[4096,512]{1,0:T(8,128)} async-done(((f32[4096,512]{1,0:T(8,128)}), f32[4096,512]{1,0:T(8,128)}) %all-reduce.33.cloned.1.call-update) | async-done | bytes 8388624 | tf_op jit(solution)/shard_map/psum | solution.py:161
  2664.0 45.6 %scatter_custom_fusion = f32[12576,512]{1,0:T(8,128)} fusion(f32[12576,512]{1,0:T(8,128)} %fusion.171, s32[4096]{0:T(1024)} %bitcast.320, f32[4096,512]{1,0:T(8,128)} %get-tuple-element.97, f32[4096]{0:T(1024)S(1)} %negate_multiply_fusion, f32[]{:T(128)} %constant.59.clone.1, pred[4096]{0:T(1024)(128)(4,1)S(1)} %bitcast.303), kind=kCustom, calls=%fused_computation.70 | custom fusion | flops 6291456 | bytes 34165248 | tf_op jit(solution)/shard_map/scatter-add | solution.py:166
  2733.5 508.1 %all-reduce.35.cloned.1.call-done = (f32[12576,512]{1,0:T(8,128)}, f32[2,512,384]{2,1,0:T(8,128)}, f32[2,128,512]{2,1,0:T(8,128)}, f32[2,512,512]{2,1,0:T(8,128)}, f32[2,512,512]{2,1,0:T(8,128)}) async-done(((f32[12576,512]{1,0:T(8,128)}, f32[2,512,384]{2,1,0:T(8,128)}, f32[2,128,512]{2,1,0:T(8,128)}, f32[2,512,512]{2,1,0:T(8,128)}, f32[2,512,512]{2,1,0:T(8,128)}), (f32[12576,512]{1,0:T(8,128)}, ...) | async-done | bytes 32047120 | tf_op jit(solution)/shard_map/psum | solution.py:189
  3275.9 64.9 %fusion.188 = (bf16[12576,512]{1,0:T(8,128)(2,1)}, f32[12576,512]{1,0:T(8,128)}, f32[12576,512]{1,0:T(8,128)}, f32[12576,512]{1,0:T(8,128)}) fusion(f32[12576,512]{1,0:T(8,128)} %param.29, f32[12576,512]{1,0:T(8,128)} %get-tuple-element.57, f32[]{:T(128)S(6)} %min.22, f32[12576,512]{1,0:T(8,128)} %param.37, f32[12576,512]{1,0:T(8,128)} %param.45), kind=kLoop, calls=%fused_computation.300 | loop fusion | flops 109461504 | bytes 193167360 | tf_op jit(solution)/shard_map/convert_element_type | solution.py:197
  (592 shorter events, 602.9 us)
Async XLA Ops:
  7.2 214.1 %all-reduce.15.cloned.1.call-start = ((), (), s32[]{:S(2)}) async-start(), calls=%async_computation | async-start | bytes 16777216 | tf_op jit(solution)/shard_map/psum | solution.py:85
  54.3 410.2 %all-reduce.17.cloned.1.call-start = ((), (), s32[]{:S(2)}) async-start(), calls=%async_computation.1 | async-start | bytes 16777216 | tf_op jit(solution)/shard_map/psum | solution.py:100
  54.5 186.4 %copy-start.51 = (bf16[2,512,384]{2,1,0:T(8,128)(2,1)}, bf16[2,512,384]{2,1,0:T(8,128)(2,1)S(1)}, u32[]{:S(2)}) copy-start(bf16[2,512,384]{2,1,0:T(8,128)(2,1)S(1)} %convert_element_type.164) | copy-start | bytes 2359300
  55.3 664.2 %copy-start.55 = (bf16[2,128,512]{2,1,0:T(8,128)(2,1)}, bf16[2,128,512]{2,1,0:T(8,128)(2,1)S(1)}, u32[]{:S(2)}) copy-start(bf16[2,128,512]{2,1,0:T(8,128)(2,1)S(1)} %convert_element_type.170) | copy-start | bytes 786436
  57.9 178.1 %copy-start.136 = (f32[1,512]{1,0:T(1,128)}, f32[1,512]{1,0:T(1,128)S(1)}, u32[]{:S(2)}) copy-start(f32[1,512]{1,0:T(1,128)S(1)} %get-tuple-element.142) | copy-start | bytes 6148
  58.0 406.5 %copy-start.99 = (f32[1,512]{1,0:T(1,128)}, f32[1,512]{1,0:T(1,128)S(1)}, u32[]{:S(2)}) copy-start(f32[1,512]{1,0:T(1,128)S(1)} %get-tuple-element.144) | copy-start | bytes 6148
  58.0 406.5 %copy-start.117 = (f32[1,512]{1,0:T(1,128)}, f32[1,512]{1,0:T(1,128)S(1)}, u32[]{:S(2)}) copy-start(f32[1,512]{1,0:T(1,128)S(1)} %get-tuple-element.143) | copy-start | bytes 6148
  58.0 415.3 %copy-start.128 = (f32[1,512]{1,0:T(1,128)}, f32[1,512]{1,0:T(1,128)S(1)}, u32[]{:S(2)}) copy-start(f32[1,512]{1,0:T(1,128)S(1)} %get-tuple-element.139) | copy-start | bytes 6148
  58.0 609.3 %copy-start.130 = (f32[1,512]{1,0:T(1,128)}, f32[1,512]{1,0:T(1,128)S(1)}, u32[]{:S(2)}) copy-start(f32[1,512]{1,0:T(1,128)S(1)} %get-tuple-element.136) | copy-start | bytes 6148
  225.3 239.1 %copy-start.65 = (f32[4096]{0:T(1024)}, f32[4096]{0:T(1024)S(1)}, u32[]{:S(2)}) copy-start(f32[4096]{0:T(1024)S(1)} %broadcast_multiply_fusion.6) | copy-start | bytes 49156
  230.0 234.4 %copy-start.67 = (f32[4096]{0:T(1024)}, f32[4096]{0:T(1024)S(1)}, u32[]{:S(2)}) copy-start(f32[4096]{0:T(1024)S(1)} %fusion.151) | copy-start | bytes 49156
  299.6 352.3 %all-reduce.19.cloned.1.call-start = ((), (), s32[]{:S(2)}) async-start(), calls=%async_computation.2 | async-start | bytes 16777216 | tf_op jit(solution)/shard_map/psum | solution.py:107
  299.8 178.4 %copy-start.69 = (bf16[2,512,512]{2,1,0:T(8,128)(2,1)}, bf16[2,512,512]{2,1,0:T(8,128)(2,1)S(1)}, u32[]{:S(2)}) copy-start(bf16[2,512,512]{2,1,0:T(8,128)(2,1)S(1)} %convert_element_type.174) | copy-start | bytes 3145732
  301.9 176.3 %copy-start.165 = (f32[1,512]{1,0:T(1,128)}, f32[1,512]{1,0:T(1,128)S(1)}, u32[]{:S(2)}) copy-start(f32[1,512]{1,0:T(1,128)S(1)} %get-tuple-element.149) | copy-start | bytes 6148
  301.9 610.7 %copy-start.168 = (f32[1,512]{1,0:T(1,128)}, f32[1,512]{1,0:T(1,128)S(1)}, u32[]{:S(2)}) copy-start(f32[1,512]{1,0:T(1,128)S(1)} %get-tuple-element.148) | copy-start | bytes 6148
  487.0 403.1 %all-reduce.21.cloned.1.call-start = ((), (), s32[]{:S(2)}) async-start(), calls=%async_computation.3 | async-start | bytes 16777216 | tf_op jit(solution)/shard_map/psum | solution.py:100
  725.2 361.0 %all-reduce.23.cloned.1.call-start = ((), (), s32[]{:S(2)}) async-start(), calls=%async_computation.4 | async-start | bytes 16777216 | tf_op jit(solution)/shard_map/psum | solution.py:107
  921.3 680.6 %all-reduce.25.cloned.1.call-start = ((), (), s32[]{:S(2)}) async-start(), calls=%async_computation.5 | async-start | bytes 16777216 | tf_op jit(solution)/shard_map/psum | solution.py:124
  1437.4 360.5 %all-reduce.27.cloned.1.call-start = ((), (), s32[]{:S(2)}) async-start(), calls=%async_computation.6 | async-start | bytes 16777216 | tf_op jit(solution)/shard_map/psum | solution.py:144
  1616.5 195.8 %copy-start.121 = (f32[4096]{0:T(1024)}, f32[4096]{0:T(1024)S(1)}, u32[]{:S(2)}) copy-start(f32[4096]{0:T(1024)S(1)} %negate_multiply_fusion.5) | copy-start | bytes 49156
  1633.0 483.5 %all-reduce.29.cloned.1.call-start = ((), (), s32[]{:S(2)}) async-start(), calls=%async_computation.7 | async-start | bytes 16777216 | tf_op jit(solution)/shard_map/psum | solution.py:161
  1951.6 366.4 %all-reduce.31.cloned.1.call-start = ((), (), s32[]{:S(2)}) async-start(), calls=%async_computation.8 | async-start | bytes 16777216 | tf_op jit(solution)/shard_map/psum | solution.py:144
  2153.1 482.4 %all-reduce.33.cloned.1.call-start = ((), (), s32[]{:S(2)}) async-start(), calls=%async_computation.9 | async-start | bytes 16777216 | tf_op jit(solution)/shard_map/psum | solution.py:161
  2470.6 771.0 %all-reduce.35.cloned.1.call-start = ((), (), s32[]{:S(2)}) async-start(), calls=%async_computation.10 | async-start | bytes 64094208 | tf_op jit(solution)/shard_map/psum | solution.py:189
  (185 other events, 5752.7 us)
Sparse Core Ops, SparseCore 0:
  54.4 166.8 all-reduce.14
  299.7 164.7 all-reduce.16
  487.1 164.7 all-reduce.18
  725.3 164.7 all-reduce.20
  921.4 164.7 all-reduce.22
  1437.5 164.4 all-reduce.24
  1633.1 164.7 all-reduce.26
  1951.7 164.7 all-reduce.28
  2153.2 164.7 all-reduce.30
  2470.7 164.7 all-reduce.32
  2709.8 531.8 all-reduce.34
where the time goes:
time: 3370 us
  waiting for transfers between devices  2040 us (61%)
  matrix products  611 us (18%)
  other arithmetic  530 us (16%)
  local copies, waits for them, and re-layouts  102 us (3%)
  blocking collectives  55.5 us (2%)
    psum x1, waiting for transfers between devices, device_step(): grads = [lax.psum(grad_arr, 'dp') for grad_arr in grads]  508 us
    psum x2, waiting for transfers between devices, local_grads(): lax.psum(lax.dot_general(d_pre_b, wup_b[layer], CONTRACT_COLS, preferred_...  329 us
    psum x2, waiting for transfers between devices, local_grads(): lax.psum(jnp.dot(hidden, wdown_b[layer], preferred_element_type=jnp.float...  329 us
    psum x2, waiting for transfers between devices, local_grads(): lax.psum(jnp.dot(context, wout_b[layer], preferred_element_type=jnp.float...  327 us
    psum x2, waiting for transfers between devices, local_grads(): lax.psum(lax.dot_general(d_qkv_b, wqkv_b[layer], CONTRACT_COLS, preferred...  227 us
    psum x1, waiting for transfers between devices, local_grads(): lax.psum(jnp.dot(d_logits, emb_b, preferred_element_type=jnp.float32), 'tp')  165 us
    psum x1, waiting for transfers between devices, local_grads(): lax.psum(jnp.where(in_shard[:, None], picked.astype(jnp.float32), 0.0), '...  158 us
    convert_element_type x1, other arithmetic, local_grads(): ((shifted / sum_exp[:, None] - onehot.astype(jnp.float32)) / n_total).ast...  98.2 us
  transfers between devices with their start and end apart: 11, of which 11 were waited for; matrix products, arithmetic and copies ran while one was open for 4% of the time, Pallas kernels for 0%

commit v1 on v0

v1 whole, which is shorter than its diff:
```python
import functools
import math
import jax
import jax.numpy as jnp
from jax import lax
from jax.experimental import pallas as pl
from jax.experimental.pallas import tpu as pltpu
from jax.sharding import PartitionSpec as P

LN_EPS = 1e-5
CLIP_NORM = 1.0
BETA_ONE = 0.9
BETA_TWO = 0.95
ADAM_EPS = 1e-8
WEIGHT_DECAY = 0.1
LEARN_RATE = 1e-3
STEP_COUNT = 10
DECAYED = (True, False, True, False, True, True, False, True)
PARAM_SPECS = (P('tp', None), P(None, None), P(None, None, 'tp'), P(None, 'tp', None), P(None, 'tp', None), P(None, None, 'tp'), P(None, 'tp'), P(None, 'tp', None))
ALL = ('tp', 'dp')
F32 = jnp.float32
BF16 = jnp.bfloat16
NN = (((1,), (0,)), ((), ()))
NT = (((1,), (1,)), ((), ()))
TN = (((0,), (0,)), ((), ()))
CHUNKS = 4
HEAD_TOK = 512
VOC_BLK = 256
Q_BLK = 256
PAD_ROWS = 8
VMEM_CAP = 60 * 1024 * 1024


def alibi_slopes(heads):
    closest = 2 ** int(math.floor(math.log2(heads)))
    first_base = 2.0 ** (-8.0 / closest)
    slopes = [first_base ** (head_idx + 1) for head_idx in range(closest)]
    extra_base = 2.0 ** (-4.0 / closest)
    extra_count = min(closest, heads - closest)
    return slopes + [extra_base ** (2 * head_idx + 1) for head_idx in range(extra_count)]


def layer_norm(values, gain, bias):
    centred = values - jnp.mean(values, axis=-1, keepdims=True)
    variance = jnp.mean(centred * centred, axis=-1, keepdims=True)
    return centred * lax.rsqrt(variance + LN_EPS) * gain + bias


def gelu_tanh(values):
    return jax.nn.gelu(values, approximate=True)


def adam_update(master, grad_arr, moment, velocity, decayed):
    mom_new = BETA_ONE * moment + (1.0 - BETA_ONE) * grad_arr
    vel_new = BETA_TWO * velocity + (1.0 - BETA_TWO) * grad_arr * grad_arr
    mom_hat = mom_new / (1.0 - BETA_ONE ** STEP_COUNT)
    vel_hat = vel_new / (1.0 - BETA_TWO ** STEP_COUNT)
    direction = mom_hat / (jnp.sqrt(vel_hat) + ADAM_EPS)
    if decayed:
        direction = direction + WEIGHT_DECAY * master
    return master - LEARN_RATE * direction, mom_new, vel_new


def mm(lhs, rhs, dims=NN):
    return lax.dot_general(lhs, rhs, dims, preferred_element_type=F32)


def stats_kernel(voc, lab_ref, x_ref, e_ref, m_ref, s_ref, t_ref):
    xb = x_ref[...].astype(BF16)
    lab = lab_ref[...]
    tok = xb.shape[0]
    full = voc // VOC_BLK

    def block(start, rows, carry):
        run_max, run_sum, run_tgt = carry
        logits = mm(e_ref[pl.ds(start, rows), :], xb, NT)
        row = lax.broadcasted_iota(jnp.int32, (rows, tok), 0) + start
        run_tgt = run_tgt + jnp.sum(jnp.where(row == lab, logits, 0.0), axis=0, keepdims=True)
        if rows != VOC_BLK:
            logits = jnp.where(row < voc, logits, -jnp.inf)
        new_max = jnp.maximum(run_max, jnp.max(logits, axis=0, keepdims=True))
        run_sum = run_sum * jnp.exp(run_max - new_max) + jnp.sum(jnp.exp(logits - new_max), axis=0, keepdims=True)
        return new_max, run_sum, run_tgt

    carry = (jnp.full((1, tok), -jnp.inf, F32), jnp.zeros((1, tok), F32), jnp.zeros((1, tok), F32))
    carry = lax.fori_loop(0, full, lambda idx, c: block(pl.multiple_of(idx * VOC_BLK, VOC_BLK), VOC_BLK, c), carry)
    tail = e_ref.shape[0] - full * VOC_BLK
    if tail:
        carry = block(full * VOC_BLK, tail, carry)
    m_ref[...], s_ref[...], t_ref[...] = carry


def head_stats(lab, x_all, e_pad, voc):
    tok, width = x_all.shape
    vec = pl.BlockSpec((1, HEAD_TOK), lambda i: (0, i))
    out = jax.ShapeDtypeStruct((1, tok), F32)
    return pl.pallas_call(
        functools.partial(stats_kernel, voc),
        grid=(tok // HEAD_TOK,),
        in_specs=[vec, pl.BlockSpec((HEAD_TOK, width), lambda i: (i, 0)), pl.BlockSpec(e_pad.shape, lambda i: (0, 0))],
        out_specs=[vec, vec, vec],
        out_shape=[out, out, out],
        compiler_params=pltpu.CompilerParams(vmem_limit_bytes=VMEM_CAP),
        cost_estimate=pl.CostEstimate(flops=2 * tok * voc * width, bytes_accessed=tok * width * 4 + voc * width * 2, transcendentals=tok * voc),
        name='head_stats',
    )(lab, x_all, e_pad)


def hgrad_kernel(voc, inv_n, first, *refs):
    if first:
        lab_ref, lse_ref, x_ref, e_ref, et_ref, g_ref, dh_ref, acc_ref = refs
    else:
        lab_ref, lse_ref, x_ref, e_ref, et_ref, gin_ref, g_ref, dh_ref, acc_ref = refs
    xb = x_ref[...].astype(BF16)
    lab = lab_ref[...]
    lse = lse_ref[...]
    tok = xb.shape[0]
    full = voc // VOC_BLK

    @pl.when(pl.program_id(0) == 0)
    def _():
        if first:
            g_ref[...] = jnp.zeros_like(g_ref)
        else:
            g_ref[...] = gin_ref[...]

    acc_ref[...] = jnp.zeros_like(acc_ref)

    def block(start, rows, keep):
        logits = mm(e_ref[pl.ds(start, rows), :], xb, NT)
        row = lax.broadcasted_iota(jnp.int32, (rows, tok), 0) + start
        prob = jnp.exp(logits - lse)
        grad = jnp.where(row == lab, prob - 1.0, prob) * inv_n
        if rows != VOC_BLK:
            grad = jnp.where(row < voc, grad, 0.0)
        grad = grad.astype(BF16)
        gemb = mm(grad, xb)
        g_ref[pl.ds(start, keep), :] += gemb[:keep]
        acc_ref[...] += mm(et_ref[:, pl.ds(start, rows)], grad)

    def body(idx, carry):
        block(pl.multiple_of(idx * VOC_BLK, VOC_BLK), VOC_BLK, VOC_BLK)
        return carry

    lax.fori_loop(0, full, body, 0)
    tail = e_ref.shape[0] - full * VOC_BLK
    if tail:
        block(full * VOC_BLK, tail, voc - full * VOC_BLK)
    dh_ref[...] = acc_ref[...].T


def head_grads(lab, lse, x_all, e_pad, e_tr, g_in, voc, inv_n):
    tok, width = x_all.shape
    first = g_in is None
    vec = pl.BlockSpec((1, HEAD_TOK), lambda i: (0, i))
    rows = pl.BlockSpec((HEAD_TOK, width), lambda i: (i, 0))
    whole = pl.BlockSpec((voc, width), lambda i: (0, 0))
    in_specs = [vec, vec, rows, pl.BlockSpec(e_pad.shape, lambda i: (0, 0)), pl.BlockSpec(e_tr.shape, lambda i: (0, 0))]
    args = [lab, lse, x_all, e_pad, e_tr]
    if not first:
        in_specs.append(whole)
        args.append(g_in)
    return pl.pallas_call(
        functools.partial(hgrad_kernel, voc, inv_n, first),
        grid=(tok // HEAD_TOK,),
        in_specs=in_specs,
        out_specs=[whole, rows],
        out_shape=[jax.ShapeDtypeStruct((voc, width), F32), jax.ShapeDtypeStruct((tok, width), F32)],
        scratch_shapes=[pltpu.VMEM((width, HEAD_TOK), F32)],
        input_output_aliases={} if first else {5: 0},
        compiler_params=pltpu.CompilerParams(vmem_limit_bytes=VMEM_CAP),
        cost_estimate=pl.CostEstimate(flops=6 * tok * voc * width, bytes_accessed=tok * width * 8 + voc * width * 12, transcendentals=tok * voc),
        name='head_grads',
    )(*args)


def probs_tr(query, key_blk, slope, scale, q_start):
    keys = key_blk.shape[0]
    rows = query.shape[0]
    key_pos = lax.broadcasted_iota(jnp.int32, (keys, rows), 0)
    qry_pos = lax.broadcasted_iota(jnp.int32, (keys, rows), 1) + q_start
    rel = key_pos - qry_pos
    scores = mm(key_blk, query, NT) * scale + slope * rel.astype(F32)
    scores = jnp.where(rel <= 0, scores, -jnp.inf)
    shifted = jnp.exp(scores - jnp.max(scores, axis=0, keepdims=True))
    return shifted / jnp.sum(shifted, axis=0, keepdims=True)


def attn_fwd_kernel(scale, head_dim, slope_ref, qkv_ref, ctx_ref):
    seq = qkv_ref.shape[0]
    for sub in range(2):
        slope = slope_ref[pl.program_id(0) * 2 + sub]
        base = sub * 3 * head_dim
        value_tr = qkv_ref[:, base + 2 * head_dim:base + 3 * head_dim].T
        for q_start in range(0, seq, Q_BLK):
            keys = q_start + Q_BLK
            query = qkv_ref[q_start:keys, base:base + head_dim]
            key_blk = qkv_ref[0:keys, base + head_dim:base + 2 * head_dim]
            probs = probs_tr(query, key_blk, slope, scale, q_start)
            ctx_tr = mm(value_tr[:, 0:keys], probs.astype(BF16))
            ctx_ref[q_start:keys, sub * head_dim:(sub + 1) * head_dim] = ctx_tr.T.astype(BF16)


def attn_bwd_kernel(scale, head_dim, slope_ref, qkv_ref, dctx_ref, out_ref):
    seq = qkv_ref.shape[0]
    out_ref[...] = jnp.zeros_like(out_ref)
    for sub in range(2):
        slope = slope_ref[pl.program_id(0) * 2 + sub]
        base = sub * 3 * head_dim
        q_cols = slice(base, base + head_dim)
        k_cols = slice(base + head_dim, base + 2 * head_dim)
        v_cols = slice(base + 2 * head_dim, base + 3 * head_dim)
        key_tr = qkv_ref[:, k_cols].T
        for q_start in range(0, seq, Q_BLK):
            keys = q_start + Q_BLK
            query = qkv_ref[q_start:keys, q_cols]
            key_blk = qkv_ref[0:keys, k_cols]
            value_blk = qkv_ref[0:keys, v_cols]
            dctx = dctx_ref[q_start:keys, sub * head_dim:(sub + 1) * head_dim]
            probs = probs_tr(query, key_blk, slope, scale, q_start)
            d_probs = mm(value_blk, dctx, NT)
            inner = jnp.sum(probs * d_probs, axis=0, keepdims=True)
            d_scores = (probs * (d_probs - inner) * scale).astype(BF16)
            out_ref[0:keys, v_cols] += mm(probs.astype(BF16), dctx)
            out_ref[0:keys, k_cols] += mm(d_scores, query)
            out_ref[q_start:keys, q_cols] = mm(key_tr[:, 0:keys], d_scores).T


def attn_forward(qkv, slopes, heads, head_dim):
    seq = qkv.shape[0]
    return pl.pallas_call(
        functools.partial(attn_fwd_kernel, head_dim ** -0.5, head_dim),
        grid=(heads // 2,),
        in_specs=[pl.BlockSpec(memory_space=pltpu.SMEM), pl.BlockSpec((seq, 6 * head_dim), lambda i: (0, i))],
        out_specs=pl.BlockSpec((seq, 2 * head_dim), lambda i: (0, i)),
        out_shape=jax.ShapeDtypeStruct((seq, heads * head_dim), BF16),
        compiler_params=pltpu.CompilerParams(vmem_limit_bytes=VMEM_CAP),
        cost_estimate=pl.CostEstimate(flops=16 * heads * seq * seq * head_dim, bytes_accessed=seq * heads * head_dim * 8, transcendentals=heads * seq * seq),
        name='attn_fwd',
    )(slopes, qkv)


def attn_backward(qkv, dctx, slopes, heads, head_dim):
    seq = qkv.shape[0]
    return pl.pallas_call(
        functools.partial(attn_bwd_kernel, head_dim ** -0.5, head_dim),
        grid=(heads // 2,),
        in_specs=[pl.BlockSpec(memory_space=pltpu.SMEM), pl.BlockSpec((seq, 6 * head_dim), lambda i: (0, i)), pl.BlockSpec((seq, 2 * head_dim), lambda i: (0, i))],
        out_specs=pl.BlockSpec((seq, 6 * head_dim), lambda i: (0, i)),
        out_shape=jax.ShapeDtypeStruct((seq, 3 * heads * head_dim), F32),
        compiler_params=pltpu.CompilerParams(vmem_limit_bytes=VMEM_CAP),
        cost_estimate=pl.CostEstimate(flops=40 * heads * seq * seq * head_dim, bytes_accessed=seq * heads * head_dim * 20, transcendentals=heads * seq * seq),
        name='attn_bwd',
    )(slopes, qkv, dctx)


def lookup_kernel(blk_rows, ids_ref, perm_ref, bound_ref, d_hbm, g_ref, out_ref, sq_ref, d_ref, sem):
    blk = pl.program_id(0)

    @pl.when(blk == 0)
    def _():
        copy = pltpu.make_async_copy(d_hbm, d_ref, sem)
        copy.start()
        copy.wait()
        sq_ref[...] = jnp.zeros_like(sq_ref)

    out_ref[...] = g_ref[...]
    first = bound_ref[blk]
    last = bound_ref[blk + 1]
    base = bound_ref[bound_ref.shape[0] - 1] + blk * blk_rows

    def body(idx, carry):
        row = ids_ref[idx] - base
        out_ref[pl.ds(row, 1), :] += d_ref[pl.ds(perm_ref[idx], 1), :]
        return carry

    lax.fori_loop(first, last, body, 0)
    vals = out_ref[...]
    sq_ref[...] += jnp.sum((vals * vals).reshape(blk_rows // 8, 8, vals.shape[1]), axis=0)


def lookup_add(ids, perm, bounds, d_all, g_head, blk_rows):
    rows, width = g_head.shape
    spec = pl.BlockSpec((blk_rows, width), lambda i, *_: (i, 0))
    return pl.pallas_call(
        functools.partial(lookup_kernel, blk_rows),
        grid_spec=pltpu.PrefetchScalarGridSpec(
            num_scalar_prefetch=3,
            grid=(rows // blk_rows,),
            in_specs=[pl.BlockSpec(memory_space=pl.ANY), spec],
            out_specs=[spec, pl.BlockSpec((8, width), lambda i, *_: (0, 0))],
            scratch_shapes=[pltpu.VMEM(d_all.shape, F32), pltpu.SemaphoreType.DMA],
        ),
        out_shape=[jax.ShapeDtypeStruct((rows, width), F32), jax.ShapeDtypeStruct((8, width), F32)],
        compiler_params=pltpu.CompilerParams(vmem_limit_bytes=VMEM_CAP),
        cost_estimate=pl.CostEstimate(flops=rows * width * 40, bytes_accessed=rows * width * 8 + d_all.shape[0] * width * 4, transcendentals=0),
        name='lookup_add',
    )(ids, perm, bounds, d_all, g_head)


def pick(values, start, size, axis):
    return lax.dynamic_slice_in_dim(values, start, size, axis)


def solution(mesh):
    tp_size = mesh.shape['tp']
    dp_size = mesh.shape['dp']
    n_dev = tp_size * dp_size

    def device_step(tokens, labels, *state):
        masters = state[0:8]
        moms = state[8:16]
        vels = state[16:24]
        embedding, vec_params, w_qkv, b_qkv, w_out, w_up, b_up, w_down = masters
        tp_rank = lax.axis_index('tp')
        dp_rank = lax.axis_index('dp')
        vocab_loc, width = embedding.shape
        voc = vocab_loc // dp_size
        seq_len = tokens.shape[1]
        n_total = seq_len * tokens.shape[0] * dp_size
        layers = w_qkv.shape[0]
        head_dim = b_qkv.shape[2] // 3
        heads = b_qkv.shape[1] * tp_size
        qkv_q = w_qkv.shape[2] // dp_size
        out_q = w_out.shape[1] // dp_size
        ff_q = w_up.shape[2] // dp_size
        slopes = jnp.array(alibi_slopes(heads), dtype=F32)

        own = jnp.concatenate([pick(tokens, tp_rank, 1, 0), pick(labels, tp_rank, 1, 0)], axis=0)
        both = lax.all_gather(own, ALL)
        tok_all = both[:, 0]
        lab_all = both[:, 1]

        id_local = tokens.reshape(-1) - tp_rank * vocab_loc
        in_shard = (id_local >= 0) & (id_local < vocab_loc)
        picked = jnp.take(embedding, jnp.clip(id_local, 0, vocab_loc - 1), axis=0)
        picked = jnp.where(in_shard[:, None], lax.reduce_precision(picked, 8, 7), 0.0)
        x_embed = lax.psum_scatter(picked, 'tp', scatter_dimension=0, tiled=True)

        weights = []
        for layer in range(layers):
            bias_q = pick(b_qkv[layer].reshape(-1), dp_rank * qkv_q, qkv_q, 0)
            bias_u = pick(b_up[layer], dp_rank * ff_q, ff_q, 0)
            bias_row = jnp.concatenate([bias_q, bias_u, jnp.zeros((width - qkv_q - ff_q,), F32)])[None]
            pack = jnp.concatenate([
                pick(w_qkv[layer], dp_rank * qkv_q, qkv_q, 1).T,
                pick(w_out[layer], dp_rank * out_q, out_q, 0),
                pick(w_up[layer], dp_rank * ff_q, ff_q, 1).T,
                pick(w_down[layer], dp_rank * ff_q, ff_q, 0),
                jnp.pad(bias_row, ((0, PAD_ROWS - 1), (0, 0)))], axis=0)
            got = lax.optimization_barrier(lax.all_gather(pack, ALL))
            at = 0
            parts = []
            for rows in (qkv_q, out_q, ff_q, ff_q):
                parts.append(got[:, at:at + rows].reshape(n_dev * rows, width).astype(BF16))
                at += rows
            bias = got[:, at]
            weights.append(tuple(parts) + (bias[:, :qkv_q].reshape(-1), bias[:, qkv_q:qkv_q + ff_q].reshape(-1)))

        emb_slice = pick(embedding, dp_rank * voc, voc, 0).astype(BF16)
        voc_pad = -(-voc // 16) * 16
        e_pad = jnp.pad(emb_slice, ((0, voc_pad - voc), (0, 0)))
        e_tr = jnp.pad(emb_slice, ((0, -(-voc // 128) * 128 - voc), (0, 0))).T

        resid, ln_zero_vjp = jax.vjp(layer_norm, x_embed, vec_params[0], vec_params[1])
        saved = []
        for layer in range(layers):
            wqkv_t, wout_b, wup_t, wdown_b, bias_q, bias_u = weights[layer]
            row_base = 2 + 6 * layer
            normed_one, ln_one_vjp = jax.vjp(layer_norm, resid, vec_params[row_base], vec_params[row_base + 1])
            act_in = normed_one.astype(BF16)
            qkv = (mm(act_in, wqkv_t, NT) + bias_q).astype(BF16)
            context = attn_forward(qkv, slopes, heads, head_dim)
            mid = resid + mm(context, wout_b) + vec_params[row_base + 2]
            normed_two, ln_two_vjp = jax.vjp(layer_norm, mid, vec_params[row_base + 3], vec_params[row_base + 4])
            mlp_in = normed_two.astype(BF16)
            pre_act = mm(mlp_in, wup_t, NT) + bias_u
            act_out, gelu_vjp = jax.vjp(gelu_tanh, pre_act)
            hidden = act_out.astype(BF16)
            resid = mid + mm(hidden, wdown_b) + vec_params[row_base + 5]
            saved.append((ln_one_vjp, act_in, qkv, context, ln_two_vjp, mlp_in, gelu_vjp, hidden))

        final_row = 2 + 6 * layers
        normed_fin, ln_fin_vjp = jax.vjp(layer_norm, resid, vec_params[final_row], vec_params[final_row + 1])

        step = seq_len // CHUNKS
        lab_loc = lab_all - (tp_rank * vocab_loc + dp_rank * voc)
        x_parts = []
        lab_parts = []
        stats = []
        for part in range(CHUNKS):
            x_all = lax.all_gather(normed_fin[part * step:(part + 1) * step], ALL).reshape(n_dev * step, width)
            lab = lab_loc[:, part * step:(part + 1) * step].reshape(1, -1)
            x_parts.append(x_all)
            lab_parts.append(lab)
            stats.append(jnp.concatenate(head_stats(lab, x_all, e_pad, voc), axis=0))
        lses = []
        loss_sum = 0.0
        for pair in range(0, CHUNKS, 2):
            got = lax.all_gather(jnp.concatenate(stats[pair:pair + 2], axis=1), ALL)
            glob_max = jnp.max(got[:, 0], axis=0)
            lse = glob_max + jnp.log(jnp.sum(got[:, 1] * jnp.exp(got[:, 0] - glob_max), axis=0))
            loss_sum = loss_sum + jnp.sum(lse - jnp.sum(got[:, 2], axis=0))
            half = lse.shape[0] // 2
            lses += [lse[None, :half], lse[None, half:]]
        loss = loss_sum / n_total

        g_slice = None
        d_parts = []
        for part in range(CHUNKS):
            g_slice, d_part = head_grads(lab_parts[part], lses[part], x_parts[part], e_pad, e_tr, g_slice, voc, 1.0 / n_total)
            d_parts.append(lax.psum_scatter(d_part.reshape(n_dev, step, width), ALL, scatter_dimension=0, tiled=False))
        d_head = jnp.concatenate(d_parts, axis=0)
        g_head = lax.all_gather(g_slice, 'dp').reshape(vocab_loc, width)

        vec_grads = {}
        d_resid, vec_grads[final_row], vec_grads[final_row + 1] = ln_fin_vjp(d_head)
        summed = {}
        for layer in reversed(range(layers)):
            ln_one_vjp, act_in, qkv, context, ln_two_vjp, mlp_in, gelu_vjp, hidden = saved[layer]
            wqkv_t, wout_b, wup_t, wdown_b, _, _ = weights[layer]
            row_base = 2 + 6 * layer
            vec_grads[row_base + 5] = jnp.sum(d_resid, axis=0)
            d_out = d_resid.astype(BF16)
            g_down = mm(hidden, d_out, TN)
            d_pre = gelu_vjp(mm(d_out, wdown_b, NT))[0]
            g_bup = jnp.sum(d_pre, axis=0)
            d_pre_b = d_pre.astype(BF16)
            g_up = mm(d_pre_b, mlp_in, TN)
            d_mid_ln, vec_grads[row_base + 3], vec_grads[row_base + 4] = ln_two_vjp(mm(d_pre_b, wup_t))
            d_mid = d_resid + d_mid_ln
            vec_grads[row_base + 2] = jnp.sum(d_mid, axis=0)
            d_attn = d_mid.astype(BF16)
            g_out = mm(context, d_attn, TN)
            d_context = mm(d_attn, wout_b, NT).astype(BF16)
            d_qkv = attn_backward(qkv, d_context, slopes, heads, head_dim)
            g_bqkv = jnp.sum(d_qkv, axis=0)
            d_qkv_b = d_qkv.astype(BF16)
            g_qkv = mm(d_qkv_b, act_in, TN)
            d_res_ln, vec_grads[row_base], vec_grads[row_base + 1] = ln_one_vjp(mm(d_qkv_b, wqkv_t))
            d_resid = d_mid + d_res_ln
            bias_rows = jnp.concatenate([g_bqkv.reshape(n_dev, qkv_q), g_bup.reshape(n_dev, ff_q), jnp.zeros((n_dev, width - qkv_q - ff_q), F32)], axis=1)
            summed[layer] = jnp.concatenate([
                g_qkv.reshape(n_dev, qkv_q, width), g_out.reshape(n_dev, out_q, width),
                g_up.reshape(n_dev, ff_q, width), g_down.reshape(n_dev, ff_q, width),
                jnp.pad(bias_rows[:, None], ((0, 0), (0, PAD_ROWS - 1), (0, 0)))], axis=1)
            if layer > 0:
                summed[layer] = lax.psum_scatter(summed[layer], ALL, scatter_dimension=0, tiled=False)
        d_embed, vec_grads[0], vec_grads[1] = ln_zero_vjp(d_resid)
        d_all = lax.all_gather(d_embed, ALL).reshape(n_total, width)
        summed[0] = lax.psum_scatter(summed[0], ALL, scatter_dimension=0, tiled=False)
        vec_grad = lax.psum(jnp.stack([vec_grads[row] for row in range(final_row + 2)]), ALL)

        blk_rows = vocab_loc // 12
        ids, perm = lax.sort((tok_all.reshape(-1), lax.iota(jnp.int32, n_total)), num_keys=1)
        edges = tp_rank * vocab_loc + jnp.arange(13, dtype=jnp.int32) * blk_rows
        bounds = jnp.sum((tok_all.reshape(-1)[None] < edges[:, None]).astype(jnp.int32), axis=1)
        bounds = jnp.concatenate([bounds, edges[:1]])
        g_emb, sq_emb = lookup_add(ids, perm, bounds, d_all, g_head, blk_rows)

        sq_dev = jnp.sum(sq_emb) / dp_size + sum(jnp.sum(summed[layer] * summed[layer]) for layer in range(layers))
        sq_total = lax.psum(sq_dev, ALL) + jnp.sum(vec_grad * vec_grad)
        clip_coef = jnp.minimum(1.0, CLIP_NORM / (jnp.sqrt(sq_total) + 1e-6))

        per_layer = []
        for layer in range(layers):
            got = lax.all_gather(summed[layer], 'dp')
            at = 0
            parts = []
            for rows in (qkv_q, out_q, ff_q, ff_q):
                parts.append(got[:, at:at + rows].reshape(dp_size * rows, width))
                at += rows
            bias = got[:, at]
            per_layer.append((parts[0].T, bias[:, :qkv_q].reshape(b_qkv.shape[1:]), parts[1], parts[2].T, bias[:, qkv_q:qkv_q + ff_q].reshape(-1), parts[3]))
        grads = [g_emb, vec_grad] + [jnp.stack([per_layer[layer][slot] for layer in range(layers)]) for slot in range(6)]
        updated = [adam_update(masters[slot], grads[slot] * clip_coef, moms[slot], vels[slot], DECAYED[slot]) for slot in range(8)]
        new_masters = [entry[0] for entry in updated]
        new_moms = [entry[1] for entry in updated]
        new_vels = [entry[2] for entry in updated]
        new_bf16 = [entry.astype(BF16) for entry in new_masters]
        return (loss, *new_masters, *new_moms, *new_vels, *new_bf16)

    data_spec = P('dp', None)
    return jax.shard_map(device_step, mesh=mesh, in_specs=(data_spec, data_spec) + PARAM_SPECS * 3, out_specs=(P(),) + PARAM_SPECS * 4, check_vma=False)
```

time: 3370 us -> 2060 us (0.61)
  waiting for transfers between devices: 2040 us -> 888 us
  Pallas kernels: 0 us -> 699 us
  matrix products: 611 us -> 95.1 us
  other arithmetic: 530 us -> 168 us
  local copies, waits for them, and re-layouts: 102 us -> 137 us
    psum x11 -> x0, waiting for transfers between devices: 2040 us -> none  [the longest x1 508 us: device_step(): grads = [lax.psum(grad_arr, 'dp') for grad_arr in grads]]
    pallas_call x0 -> x13, Pallas kernels: none -> 699 us  [the longest x4 341 us: head_grads(): pl.pallas_call(functools.partial(hgrad_kernel, voc, inv_n, first), grid=(...]
    reduce_scatter x0 -> x7, waiting for transfers between devices: none -> 560 us  [the longest x4 185 us: device_step(): lax.psum_scatter(d_part.reshape(n_dev, step, width), ALL, scatter_dimensi...]
    dot_general x37 -> x24, matrix products: 570 us -> 95.1 us  [mm(): return lax.dot_general(lhs, rhs, dims, preferred_element_type=F32)]
    all_gather x0 -> x12, waiting for transfers between devices: none -> 325 us  [the longest x1 139 us: device_step(): g_head = lax.all_gather(g_slice, 'dp').reshape(vocab_loc, width)]
    convert_element_type x20 -> x8, other arithmetic: 215 us -> 85 us  [device_step(): new_bf16 = [entry.astype(BF16) for entry in new_masters]]
    reduce_sum x15 -> x14, other arithmetic: 93.8 us -> 15.9 us  [the longest x2 6.4 us: device_step(): g_bqkv = jnp.sum(d_qkv, axis=0)]
    reduce_sum x12 -> x8, other arithmetic: 82.4 us -> 8.78 us  [layer_norm(): centred = values - jnp.mean(values, axis=-1, keepdims=True)]
  transfers between devices with their start and end apart: 11 -> 19, of which waited for: 11 -> 12; matrix products, arithmetic and copies ran while one was open for 4% -> 6% of each run, Pallas kernels for 0% -> 26%
where the time goes in v1:
time: 2060 us
  waiting for transfers between devices  888 us (43%)
  Pallas kernels  699 us (34%)
  other arithmetic  168 us (8%)
  local copies, waits for them, and re-layouts  137 us (7%)
  matrix products  95.1 us (5%)
  blocking collectives  45.5 us (2%)
  between operations  24.1 us (1%)
    pallas_call x4, Pallas kernels, head_grads(): pl.pallas_call(functools.partial(hgrad_kernel, voc, inv_n, first), grid=(...  341 us
    pallas_call x4, Pallas kernels, head_stats(): pl.pallas_call(functools.partial(stats_kernel, voc), grid=(tok // HEAD_TO...  199 us
    reduce_scatter x4, waiting for transfers between devices, device_step(): lax.psum_scatter(d_part.reshape(n_dev, step, width), ALL, scatter_dimensi...  185 us
    reduce_scatter x1, waiting for transfers between devices, device_step(): lax.psum_scatter(summed[layer], ALL, scatter_dimension=0, tiled=False)  155 us
    all_gather x1, waiting for transfers between devices, device_step(): g_head = lax.all_gather(g_slice, 'dp').reshape(vocab_loc, width)  139 us
    all_gather x1, waiting for transfers between devices, device_step(): d_all = lax.all_gather(d_embed, ALL).reshape(n_total, width)  134 us
    reduce_scatter x1, waiting for transfers between devices, device_step(): lax.psum_scatter(summed[0], ALL, scatter_dimension=0, tiled=False)  111 us
    reduce_scatter x1, waiting for transfers between devices, device_step(): x_embed = lax.psum_scatter(picked, 'tp', scatter_dimension=0, tiled=True)  109 us
  transfers between devices with their start and end apart: 19, of which 12 were waited for; matrix products, arithmetic and copies ran while one was open for 6% of the time, Pallas kernels for 26%

profile of v1, /device:TPU:0, one launch (start us, length us, event | category | flops | bytes accessed | tf_op | source)
XLA Modules:
  0.0 2059.4 jit_solution(3023171588668964780)
XLA Ops:
  9.7 26.2 %gather_fusion = f32[4096,512]{1,0:T(8,128)} fusion(f32[12576,512]{1,0:T(8,128)} %param.29, s32[4096]{0:T(1024)S(1)} %broadcast_clamp_fusion), kind=kCustom, calls=%fused_computation | custom fusion | bytes 16793600 | tf_op jit(solution)/shard_map/jit(_take)/gather | solution.py:336
  55.8 108.5 %reduce-scatter.8.cloned.1.call-done = f32[1024,512]{1,0:T(8,128)} async-done(((f32[4096,512]{1,0:T(8,128)}), f32[1024,512]{1,0:T(8,128)}) %reduce-scatter.8.cloned.1.call-update) | async-done | bytes 2097168 | tf_op jit(solution)/shard_map/reduce_scatter | solution.py:338
  178.1 36.3 %all-gather.31.cloned.1.call-done = f32[6272,512]{1,0:T(8,128)} async-done(((f32[392,512]{1,0:T(8,128)}), f32[6272,512]{1,0:T(8,128)}) %all-gather.31.cloned.1.call-update) | async-done | bytes 12845072 | tf_op jit(solution)/shard_map/all_gather | solution.py:351
  242.0 20.1 attn_fwd.2
  278.3 20.4 attn_fwd.3
  363.5 49.7 %head_stats.4 = (f32[1,4096]{1,0:T(1,128)}, f32[1,4096]{1,0:T(1,128)}, f32[1,4096]{1,0:T(1,128)}) custom-call(s32[1,4096]{1,0:T(1,128)} %bitcast.322, f32[4096,512]{1,0:T(8,128)} %all-gather.35.cloned.1.call-done.x_ref.refs_2_, bf16[3152,512]{1,0:T(8,128)(2,1)} %pad.24.clone.e_ref.refs_3_), custom_call_target="tpu_custom_call" | custom-call | flops 13186891776 | bytes 11608064 | tf_op jit(solution)/shard_map/head_stats/pallas_call | solution.py:97
  415.1 49.7 %head_stats.5 = (f32[1,4096]{1,0:T(1,128)}, f32[1,4096]{1,0:T(1,128)}, f32[1,4096]{1,0:T(1,128)}) custom-call(s32[1,4096]{1,0:T(1,128)} %bitcast.320, f32[4096,512]{1,0:T(8,128)} %all-gather.37.cloned.1.call-done.x_ref.refs_2_, bf16[3152,512]{1,0:T(8,128)(2,1)} %pad.24.clone.e_ref.refs_3_), custom_call_target="tpu_custom_call" | custom-call | flops 13186891776 | bytes 11608064 | tf_op jit(solution)/shard_map/head_stats/pallas_call | solution.py:97
  466.7 49.7 %head_stats.7 = (f32[1,4096]{1,0:T(1,128)}, f32[1,4096]{1,0:T(1,128)}, f32[1,4096]{1,0:T(1,128)}) custom-call(s32[1,4096]{1,0:T(1,128)} %bitcast.316, f32[4096,512]{1,0:T(8,128)} %all-gather.41.cloned.1.call-done.x_ref.refs_2_, bf16[3152,512]{1,0:T(8,128)(2,1)} %pad.24.clone.e_ref.refs_3_), custom_call_target="tpu_custom_call" | custom-call | flops 13186891776 | bytes 11608064 | tf_op jit(solution)/shard_map/head_stats/pallas_call | solution.py:97
  518.3 49.7 %head_stats.6 = (f32[1,4096]{1,0:T(1,128)}, f32[1,4096]{1,0:T(1,128)}, f32[1,4096]{1,0:T(1,128)}) custom-call(s32[1,4096]{1,0:T(1,128)} %bitcast.318, f32[4096,512]{1,0:T(8,128)} %all-gather.39.cloned.1.call-done.x_ref.refs_2_, bf16[3152,512]{1,0:T(8,128)(2,1)} %pad.24.clone.e_ref.refs_3_), custom_call_target="tpu_custom_call" | custom-call | flops 13186891776 | bytes 11608064 | tf_op jit(solution)/shard_map/head_stats/pallas_call | solution.py:97
  576.4 83.8 %head_grads.4 = (f32[3144,512]{1,0:T(8,128)}, f32[4096,512]{1,0:T(8,128)}) custom-call(s32[1,4096]{1,0:T(1,128)} %bitcast.323, f32[1,4096]{1,0:T(1,128)} %bitcast.327, f32[4096,512]{1,0:T(8,128)} %all-gather.35.cloned.1.call-done.x_ref.refs_2_, bf16[3152,512]{1,0:T(8,128)(2,1)} %pad.24.clone.e_ref.refs_3_, bf16[512,3200]{1,0:T(8,128)(2,1)} %pad_bitcast_fusion.refs_4_), custom_call_target="tpu_custom_call" | custom-call | flops 39560675328 | bytes 36093952 | tf_op jit(solution)/shard_map/head_grads/pallas_call | solution.py:163
  660.3 85.6 %head_grads.5 = (f32[3144,512]{1,0:T(8,128)}, f32[4096,512]{1,0:T(8,128)}) custom-call(s32[1,4096]{1,0:T(1,128)} %bitcast.321, f32[1,4096]{1,0:T(1,128)} %bitcast.324, f32[4096,512]{1,0:T(8,128)} %all-gather.37.cloned.1.call-done.x_ref.refs_2_, bf16[3152,512]{1,0:T(8,128)(2,1)} %pad.24.clone.e_ref.refs_3_, ...), custom_call_target="tpu_custom_call", output_to_operand_aliasing={{0}: (5, {})} | custom-call | flops 39560675328 | bytes 36093952 | tf_op jit(solution)/shard_map/head_grads/pallas_call | solution.py:163
  752.9 85.6 %head_grads.6 = (f32[3144,512]{1,0:T(8,128)}, f32[4096,512]{1,0:T(8,128)}) custom-call(s32[1,4096]{1,0:T(1,128)} %bitcast.319, f32[1,4096]{1,0:T(1,128)} %bitcast.326, f32[4096,512]{1,0:T(8,128)} %all-gather.39.cloned.1.call-done.x_ref.refs_2_, bf16[3152,512]{1,0:T(8,128)(2,1)} %pad.24.clone.e_ref.refs_3_, ...), custom_call_target="tpu_custom_call", output_to_operand_aliasing={{0}: (5, {})} | custom-call | flops 39560675328 | bytes 36093952 | tf_op jit(solution)/shard_map/head_grads/pallas_call | solution.py:163
  838.5 85.5 %head_grads.7 = (f32[3144,512]{1,0:T(8,128)}, f32[4096,512]{1,0:T(8,128)}) custom-call(s32[1,4096]{1,0:T(1,128)} %bitcast.317, f32[1,4096]{1,0:T(1,128)} %bitcast.325, f32[4096,512]{1,0:T(8,128)} %all-gather.41.cloned.1.call-done.x_ref.refs_2_, bf16[3152,512]{1,0:T(8,128)(2,1)} %pad.24.clone.e_ref.refs_3_, ...), custom_call_target="tpu_custom_call", output_to_operand_aliasing={{0}: (5, {})} | custom-call | flops 39560675328 | bytes 36093952 | tf_op jit(solution)/shard_map/head_grads/pallas_call | solution.py:163
  925.1 91.6 %reduce-scatter.16.cloned.1.call-done = f32[1,256,512]{2,1,0:T(8,128)} async-done(((f32[16,256,512]{2,1,0:T(8,128)}), f32[1,256,512]{2,1,0:T(8,128)}) %reduce-scatter.16.cloned.1.call-update) | async-done | bytes 524304 | tf_op jit(solution)/shard_map/reduce_scatter | solution.py:412
  1016.8 93.7 %reduce-scatter.14.cloned.1.call-done = f32[1,256,512]{2,1,0:T(8,128)} async-done(((f32[16,256,512]{2,1,0:T(8,128)}), f32[1,256,512]{2,1,0:T(8,128)}) %reduce-scatter.14.cloned.1.call-update) | async-done | bytes 524304 | tf_op jit(solution)/shard_map/reduce_scatter | solution.py:412
  1132.8 29.7 %attn_bwd.2 = f32[1024,1536]{1,0:T(8,128)} custom-call(f32[8]{0:T(128)} %constant.197.clone.slope_ref, bf16[1024,1536]{1,0:T(8,128)(2,1)} %add_convert_fusion.qkv_ref, bf16[1024,512]{1,0:T(8,128)(2,1)} %convolution_convert_fusion.1.dctx_ref), custom_call_target="tpu_custom_call" | custom-call | flops 21474836480 | bytes 10485760 | tf_op jit(solution)/shard_map/attn_bwd/pallas_call | solution.py:245
  1202.4 29.5 %attn_bwd.3 = f32[1024,1536]{1,0:T(8,128)} custom-call(f32[8]{0:T(128)} %constant.197.clone.slope_ref, bf16[1024,1536]{1,0:T(8,128)(2,1)} %add_convert_fusion.1.qkv_ref, bf16[1024,512]{1,0:T(8,128)(2,1)} %convolution_convert_fusion.dctx_ref), custom_call_target="tpu_custom_call" | custom-call | flops 21474836480 | bytes 10485760 | tf_op jit(solution)/shard_map/attn_bwd/pallas_call | solution.py:245
  1276.1 110.8 %reduce-scatter.18.cloned.1.call-done = f32[1,392,512]{2,1,0:T(8,128)} async-done(((f32[16,392,512]{2,1,0:T(8,128)}), f32[1,392,512]{2,1,0:T(8,128)}) %reduce-scatter.18.cloned.1.call-update) | async-done | bytes 802832 | tf_op jit(solution)/shard_map/reduce_scatter | solution.py:451
  1386.9 155.1 %reduce-scatter.20.cloned.1.call-done = f32[1,392,512]{2,1,0:T(8,128)} async-done(((f32[16,392,512]{2,1,0:T(8,128)}), f32[1,392,512]{2,1,0:T(8,128)}) %reduce-scatter.20.cloned.1.call-update) | async-done | bytes 802832 | tf_op jit(solution)/shard_map/reduce_scatter | solution.py:448
  1586.2 139.5 %all-gather.45.cloned.1.call-done.g_ref = f32[12576,512]{1,0:T(8,128)} async-done(((f32[3144,512]{1,0:T(8,128)}), f32[12576,512]{1,0:T(8,128)}) %all-gather.45.cloned.1.call-update) | async-done | bytes 25755664 | tf_op jit(solution)/shard_map/all_gather | solution.py:414
  1725.7 134.0 %all-gather.43.cloned.1.call-done.d_hbm = f32[16384,512]{1,0:T(8,128)} async-done(((f32[1024,512]{1,0:T(8,128)}), f32[16384,512]{1,0:T(8,128)}) %all-gather.43.cloned.1.call-update) | async-done | bytes 33554448 | tf_op jit(solution)/shard_map/all_gather | solution.py:450
  1859.6 60.2 %lookup_add.1 = (f32[12576,512]{1,0:T(8,128)}, f32[8,512]{1,0:T(8,128)}) custom-call(s32[16384]{0:T(1024)} %get-tuple-element.69.ids_ref, s32[16384]{0:T(1024)} %get-tuple-element.70.perm_ref, s32[14]{0:T(128)} %pad_add_fusion.bound_ref, f32[16384,512]{1,0:T(8,128)} %all-gather.43.cloned.1.call-done.d_hbm, f32[12576,512]{1,0:T(8,128)} %all-gather.45.cloned.1.call-done.g_ref), custom_call_target="tpu_custom_call" | custom-call | flops 257556480 | bytes 85065728 | tf_op jit(solution)/shard_map/lookup_add/pallas_call | solution.py:285
  1924.0 32.1 %all-reduce.6 = (f32[]{:T(128)}, f32[16,512]{1,0:T(8,128)S(1)}) all-reduce(f32[]{:T(128)S(6)} %add.523, f32[16,512]{1,0:T(8,128)S(1)} %stack.61), channel_id=1, replica_groups=mesh['tp'=4,'dp'=4] {'tp','dp'}, use_global_device_ids=true, to_apply=%region_48.49 | all-reduce | flops 8193 | bytes 65544 | tf_op jit(solution)/shard_map/psum | solution.py:462
  1971.5 65.5 %fusion.79 = (bf16[12576,512]{1,0:T(8,128)(2,1)}, f32[12576,512]{1,0:T(8,128)}, f32[12576,512]{1,0:T(8,128)}, f32[12576,512]{1,0:T(8,128)}) fusion(f32[12576,512]{1,0:T(8,128)} %param.29, f32[12576,512]{1,0:T(8,128)} %get-tuple-element.79, f32[]{:T(128)S(6)} %min.22, f32[12576,512]{1,0:T(8,128)} %param.37, f32[12576,512]{1,0:T(8,128)} %param.45), kind=kLoop, calls=%fused_computation.250 | loop fusion | flops 109461504 | bytes 193167360 | tf_op jit(solution)/shard_map/convert_element_type | solution.py:480
  (591 shorter events, 342.6 us)
Async XLA Ops:
  8.0 309.4 %copy-start = (s32[4,1024]{1,0:T(4,128)S(1)}, s32[4,1024]{1,0:T(4,128)}, u32[]{:S(2)}) copy-start(s32[4,1024]{1,0:T(4,128)} %param.28) | copy-start | bytes 49156
  8.1 156.3 %reduce-scatter.8.cloned.1.call-start = ((), (), s32[]{:S(2)}) async-start(), calls=%async_computation.7 | async-start | bytes 10485760 | tf_op jit(solution)/shard_map/reduce_scatter | solution.py:338
  43.4 124.9 %all-gather.33.cloned.1.call-start = ((), (), s32[]{:S(2)}) async-start(), calls=%async_computation.17 | async-start | bytes 13647872 | tf_op jit(solution)/shard_map/all_gather | solution.py:351
  53.2 161.3 %all-gather.31.cloned.1.call-start = ((), (), s32[]{:S(2)}) async-start(), calls=%async_computation.16 | async-start | bytes 13647872 | tf_op jit(solution)/shard_map/all_gather | solution.py:351
  55.5 308.1 %all-gather.35.cloned.1.call-start = ((), (), s32[]{:S(2)}) async-start(), calls=%async_computation.18 | async-start | bytes 8912896 | tf_op jit(solution)/shard_map/all_gather | solution.py:392
  55.8 217.3 %copy-start.125 = (f32[1,512]{1,0:T(1,128)}, f32[1,512]{1,0:T(1,128)S(1)}, u32[]{:S(2)}) copy-start(f32[1,512]{1,0:T(1,128)S(1)} %get-tuple-element.336) | copy-start | bytes 6148
  55.8 246.0 %copy-start.123 = (f32[1,512]{1,0:T(1,128)}, f32[1,512]{1,0:T(1,128)S(1)}, u32[]{:S(2)}) copy-start(f32[1,512]{1,0:T(1,128)S(1)} %get-tuple-element.333) | copy-start | bytes 6148
  55.8 246.0 %copy-start.141 = (f32[1,512]{1,0:T(1,128)}, f32[1,512]{1,0:T(1,128)S(1)}, u32[]{:S(2)}) copy-start(f32[1,512]{1,0:T(1,128)S(1)} %get-tuple-element.332) | copy-start | bytes 6148
  55.8 256.4 %copy-start.97 = (f32[1,512]{1,0:T(1,128)}, f32[1,512]{1,0:T(1,128)S(1)}, u32[]{:S(2)}) copy-start(f32[1,512]{1,0:T(1,128)S(1)} %get-tuple-element.330) | copy-start | bytes 6148
  314.4 100.7 %all-gather.37.cloned.1.call-start = ((), (), s32[]{:S(2)}) async-start(), calls=%async_computation.19 | async-start | bytes 8912896 | tf_op jit(solution)/shard_map/all_gather | solution.py:392
  315.2 151.6 %all-gather.41.cloned.1.call-start = ((), (), s32[]{:S(2)}) async-start(), calls=%async_computation.21 | async-start | bytes 8912896 | tf_op jit(solution)/shard_map/all_gather | solution.py:392
  315.9 202.4 %all-gather.39.cloned.1.call-start = ((), (), s32[]{:S(2)}) async-start(), calls=%async_computation.20 | async-start | bytes 8912896 | tf_op jit(solution)/shard_map/all_gather | solution.py:392
  316.6 253.0 %all-gather.47.cloned.1.call-start = ((), (), s32[]{:S(2)}) async-start(), calls=%async_computation.24 | async-start | bytes 2228224 | tf_op jit(solution)/shard_map/all_gather | solution.py:400
  466.4 279.8 %all-gather.49.cloned.1.call-start = ((), (), s32[]{:S(2)}) async-start(), calls=%async_computation.25 | async-start | bytes 2228224 | tf_op jit(solution)/shard_map/all_gather | solution.py:400
  569.5 355.6 %reduce-scatter.10.cloned.1.call-start = ((), (), s32[]{:S(2)}) async-start(), calls=%async_computation.8 | async-start | bytes 8912896 | tf_op jit(solution)/shard_map/reduce_scatter | solution.py:412
  660.2 264.9 %reduce-scatter.12.cloned.1.call-start = ((), (), s32[]{:S(2)}) async-start(), calls=%async_computation.9 | async-start | bytes 8912896 | tf_op jit(solution)/shard_map/reduce_scatter | solution.py:412
  745.9 270.8 %reduce-scatter.16.cloned.1.call-start = ((), (), s32[]{:S(2)}) async-start(), calls=%async_computation.11 | async-start | bytes 8912896 | tf_op jit(solution)/shard_map/reduce_scatter | solution.py:412
  924.0 186.5 %reduce-scatter.14.cloned.1.call-start = ((), (), s32[]{:S(2)}) async-start(), calls=%async_computation.10 | async-start | bytes 8912896 | tf_op jit(solution)/shard_map/reduce_scatter | solution.py:412
  924.8 462.1 %reduce-scatter.18.cloned.1.call-start = ((), (), s32[]{:S(2)}) async-start(), calls=%async_computation.12 | async-start | bytes 13647872 | tf_op jit(solution)/shard_map/reduce_scatter | solution.py:451
  1251.0 291.1 %reduce-scatter.20.cloned.1.call-start = ((), (), s32[]{:S(2)}) async-start(), calls=%async_computation.13 | async-start | bytes 13647872 | tf_op jit(solution)/shard_map/reduce_scatter | solution.py:448
  1276.0 297.9 %all-gather.27.cloned.1.call-start = ((), (), s32[]{:S(2)}) async-start(), calls=%async_computation.14 | async-start | bytes 4014080 | tf_op jit(solution)/shard_map/all_gather | solution.py:467
  1386.9 188.0 %all-gather.29.cloned.1.call-start = ((), (), s32[]{:S(2)}) async-start(), calls=%async_computation.15 | async-start | bytes 4014080 | tf_op jit(solution)/shard_map/all_gather | solution.py:467
  1542.1 183.6 %all-gather.45.cloned.1.call-start = ((), (), s32[]{:S(2)}) async-start(), calls=%async_computation.23 | async-start | bytes 32194560 | tf_op jit(solution)/shard_map/all_gather | solution.py:414
  1542.7 317.0 %all-gather.43.cloned.1.call-start = ((), (), s32[]{:S(2)}) async-start(), calls=%async_computation.22 | async-start | bytes 35651584 | tf_op jit(solution)/shard_map/all_gather | solution.py:450
  (157 other events, 4503.2 us)
Sparse Core Ops, SparseCore 0:
  43.5 120.7 reduce-scatter.7
  1387.0 25.5 all-gather.26
  1542.2 24.9 all-gather.28
  1568.6 157.0 all-gather.44
  1728.3 131.2 all-gather.42
Sparse Core Ops, SparseCore 1:
  53.3 87.6 all-gather.32
  143.6 70.8 all-gather.30
  314.5 49.0 all-gather.34
  366.4 48.7 all-gather.36
  418.0 48.7 all-gather.40
  469.6 48.6 all-gather.38
  521.0 28.3 all-gather.46
  569.6 28.2 all-gather.48
  660.3 92.6 reduce-scatter.9
  755.8 90.8 reduce-scatter.11
  924.1 92.6 reduce-scatter.15
  1019.7 90.8 reduce-scatter.13
  1251.1 135.7 reduce-scatter.17
  1389.7 152.3 reduce-scatter.19
